TPU v7x, 32 devices: a whole 2x2x4 slice. The times are simulated.
32 devices in a mesh: groups: 2 (over x), freq: 8 (over z, y), gvec: 2 (over core).
Axes of the slice: x: 2, y: 2, z: 4, core: 2. Of those that a mesh axis runs over, the one named last changes fastest.
Arguments:
- screened: bfloat16 [16, 3072, 3072], P(('groups', 'freq'), 'gvec'), parts along dimension 0, may hold values from -0.109375 to 0.109375
- densities: bfloat16 [6144, 512], P(('groups', 'gvec'), 'freq'), parts along dimension 0, may hold values from -0.8046875 to 0.8046875
- pair_order: int32 [512], replicated, may hold values from 0 to 511, each once
- quad_index: int32 [4, 8], replicated, may hold values from 0 to 63
- quad_table: float32 [64], replicated, may hold values from 0.05 to 0.5
Outputs:
- kernel_out: float32 [8, 512, 512], P('groups', 'freq', 'gvec'), parts along dimension 0
There are 2 independent parts, one for each index of `groups`. A program takes and returns all parts, laid end to end along the dimension named above; an argument that names none is the same for every part. Nothing has to cross between parts.
All inputs are finite; a program needn't handle non-finite values.
Results may differ from a plain program's by a relative error of at most 0.0029.
Values may be sent and summed in bfloat16 or wider, within the bound.
No kernel may reach another device: no remote copies, remote signals or barrier semaphores. Data moves between devices by JAX's collectives and lax.ppermute only.
A program may use at most 64 MiB of HBM per device.

v0:
```python
import jax
import jax.numpy as jnp
from jax import lax
from jax.sharding import PartitionSpec as P


def body(screened, densities, pair_order, quad_index, quad_table):
    screen = screened[0]
    own_rows = lax.all_gather(densities, "freq", axis=1, tiled=True)
    own_rows = jnp.take(own_rows, pair_order, axis=1)
    product = jnp.dot(
        screen,
        lax.all_gather(own_rows, "gvec", axis=0, tiled=True),
        preferred_element_type=jnp.float32,
    )
    product = product.astype(jnp.bfloat16)
    kernel = lax.dot_general(
        own_rows, product, (((0,), (0,)), ((), ())), preferred_element_type=jnp.float32
    )
    table_size = quad_table.shape[0]
    onehot = (
        quad_index[:, :, None] == jnp.arange(table_size, dtype=jnp.int32)[None, None, :]
    ).astype(jnp.float32)
    weights = jnp.sum(onehot * quad_table[None, None, :], axis=2)
    halves = lax.psum_scatter(kernel, "gvec", scatter_dimension=1, tiled=True)
    return jnp.einsum(
        "of,fij->oij",
        weights,
        lax.all_to_all(halves[None], "freq", split_axis=1, concat_axis=0, tiled=True),
        precision=lax.Precision.HIGHEST,
    )


def solution(mesh):
    placed = (P(("groups", "freq"), "gvec", None), P(("groups", "gvec"), "freq"), P(), P(), P())
    return jax.shard_map(
        body, mesh=mesh, in_specs=placed, out_specs=P("groups", "freq", "gvec"), check_vma=False
    )
```

profile of v0, /device:TPU:0, one launch (start us, length us, event | category | flops | bytes accessed | tf_op | source)
XLA Modules:
  0.0 126.2 jit_solution(10194464482765181643)
XLA Ops:
  6.5 0.0 all-gather.3.cloned.1.call-start
  6.5 0.7 all-gather.3.cloned.1.call-update
  7.3 0.0 all-gather.5.cloned.1.call-start
  7.3 0.7 compare_select_fusion
  8.0 0.7 compare_and_fusion
  8.7 47.8 %all-gather.3.cloned.1.call-done = bf16[1536,512]{0,1:T(8,128)(2,1)} async-done(((bf16[1536,64]{0,1:T(8,128)(2,1)}), bf16[1536,512]{0,1:T(8,128)(2,1)}) %all-gather.3.cloned.1.call-update) | async-done | bytes 1572880 | tf_op jit(solution)/shard_map/all_gather | solution.py:9
  56.5 5.2 %gather_fusion = bf16[512,1536]{1,0:T(8,128)(2,1)S(1)} fusion(bf16[1536,512]{0,1:T(8,128)(2,1)} %all-gather.3.cloned.1.call-done, s32[1024]{0:T(1024)S(1)} %pad_clamp_fusion), kind=kCustom, calls=%fused_computation | custom fusion | bytes 3147776 | tf_op jit(solution)/shard_map/jit(_take)/gather | solution.py:10
  61.7 1.4 %fusion.6 = bf16[1536,512]{0,1:T(8,128)(2,1)} fusion(bf16[512,1536]{1,0:T(8,128)(2,1)S(1)} %gather_fusion, pred[512]{0:T(512)(128)(4,1)S(1)} %compare_and_fusion), kind=kLoop, calls=%fused_computation.6 | loop fusion | flops 786432 | bytes 3146240 | tf_op jit(solution)/shard_map/jit(_take)/select_n | solution.py:10
  63.0 0.0 all-gather.5.cloned.1.call-update
  63.1 0.0 reduce-scatter.2.cloned.1.call-start
  63.1 10.6 %all-gather.5.cloned.1.call-done = bf16[3072,512]{0,1:T(8,128)(2,1)} async-done(((bf16[1536,512]{0,1:T(8,128)(2,1)}), bf16[3072,512]{0,1:T(8,128)(2,1)}) %all-gather.5.cloned.1.call-update) | async-done | bytes 3145744 | tf_op jit(solution)/shard_map/all_gather | solution.py:13
  73.7 11.5 %fusion.5 = f32[512,512]{1,0:T(8,128)} fusion(bf16[512,1536]{1,0:T(8,128)(2,1)S(1)} %gather_fusion, pred[512]{0:T(512)(128)(4,1)S(1)} %compare_and_fusion, bf16[3072,512]{0,1:T(8,128)(2,1)} %all-gather.5.cloned.1.call-done, bf16[1,1536,3072]{2,1,0:T(8,128)(2,1)} %param.5), kind=kOutput, calls=%fused_computation.5 | convolution fusion | flops 5638717440 | bytes 15204864 | tf_op jit(solution)/shard_map/dot_general | solution.py:17
  85.2 0.0 copy-start
  85.2 0.0 copy-start.1
  85.2 0.0 reduce-scatter.2.cloned.1.call-update
  85.2 9.7 %reduce-scatter.2.cloned.1.call-done = f32[512,256]{1,0:T(8,128)} async-done(((f32[512,512]{1,0:T(8,128)}), f32[512,256]{1,0:T(8,128)}) %reduce-scatter.2.cloned.1.call-update) | async-done | bytes 524304 | tf_op jit(solution)/shard_map/reduce_scatter | solution.py:25
  95.0 2.4 %copy.13 = f32[1,512,256]{2,0,1:T(1,128)} copy(f32[1,512,256]{2,1,0:T(8,128)} %bitcast.16) | data formatting | bytes 1048576 | tf_op jit(solution)/shard_map/broadcast_in_dim | solution.py:29
  97.3 5.8 %all-to-all-start = ((f32[1,512,256]{2,0,1:T(1,128)}), f32[1,512,256]{2,0,1:T(1,128)S(1)}, u32[]{:S(2)}, u32[]{:S(2)}) async-start(f32[1,512,256]{2,0,1:T(1,128)} %copy.13), calls=%async_computation.1 | async-start | bytes 1048576 | tf_op jit(solution)/shard_map/all_to_all | solution.py:29
  103.1 0.0 copy-done
  103.1 0.0 copy-done.1
  103.1 0.2 select_reduce_fusion
  103.3 14.8 %all-to-all-done = f32[1,512,256]{2,0,1:T(1,128)S(1)} async-done(((f32[1,512,256]{2,0,1:T(1,128)}), f32[1,512,256]{2,0,1:T(1,128)S(1)}, u32[]{:S(2)}, u32[]{:S(2)}) %all-to-all-start) | async-done | bytes 524320 | tf_op jit(solution)/shard_map/all_to_all | solution.py:29
  118.1 0.8 fusion.9
  118.9 0.8 copy.15
  (2 shorter events, 0.0 us)
Async XLA Ops:
  6.5 49.9 %all-gather.3.cloned.1.call-start = ((), (), s32[]{:S(2)}) async-start(), calls=%async_computation.2 | async-start | bytes 1769472 | tf_op jit(solution)/shard_map/all_gather | solution.py:9
  7.3 66.4 %all-gather.5.cloned.1.call-start = ((), (), s32[]{:S(2)}) async-start(), calls=%async_computation.3 | async-start | bytes 4718592 | tf_op jit(solution)/shard_map/all_gather | solution.py:13
  63.1 31.9 %reduce-scatter.2.cloned.1.call-start = ((), (), s32[]{:S(2)}) async-start(), calls=%async_computation.4 | async-start | bytes 1572864 | tf_op jit(solution)/shard_map/reduce_scatter | solution.py:25
  85.2 17.9 %copy-start = (s32[4,8]{1,0:T(4,128)S(1)}, s32[4,8]{1,0:T(4,128)}, u32[]{:S(2)}) copy-start(s32[4,8]{1,0:T(4,128)} %param.8) | copy-start | bytes 388
  85.2 17.9 %copy-start.1 = (f32[64]{0:T(128)S(1)}, f32[64]{0:T(128)}, u32[]{:S(2)}) copy-start(f32[64]{0:T(128)} %param.9) | copy-start | bytes 772
  97.3 20.7 %all-to-all-start = ((f32[1,512,256]{2,0,1:T(1,128)}), f32[1,512,256]{2,0,1:T(1,128)S(1)}, u32[]{:S(2)}, u32[]{:S(2)}) async-start(f32[1,512,256]{2,0,1:T(1,128)} %copy.13), calls=%async_computation.1 | async-start | bytes 1048576 | tf_op jit(solution)/shard_map/all_to_all | solution.py:29
Sparse Core Ops, SparseCore 0:
  9.5 46.8 all-gather.2
  63.2 10.4 all-gather.4
  85.3 9.5 reduce-scatter.1
where the time goes:
time: 126 us
  waiting for transfers between devices  83.6 us (66%)
  between operations  13.1 us (10%)
  matrix products  12.3 us (10%)
  local copies, waits for them, and re-layouts  8.37 us (7%)
  starting transfers between devices  5.84 us (5%)
  other arithmetic  2.9 us (2%)
    all_gather x1, waiting for transfers between devices, body(): own_rows = lax.all_gather(densities, 'freq', axis=1, tiled=True)  47.8 us
    all_to_all x1, waiting for transfers between devices, body(): lax.all_to_all(halves[None], 'freq', split_axis=1, concat_axis=0, tiled=T...  14.8 us
    dot_general x1, matrix products, body(): lax.dot_general(own_rows, product, (((0,), (0,)), ((), ())), preferred_el...  11.5 us
    all_gather x1, waiting for transfers between devices, body(): lax.all_gather(own_rows, 'gvec', axis=0, tiled=True)  10.6 us
    reduce_scatter x1, waiting for transfers between devices, body(): halves = lax.psum_scatter(kernel, 'gvec', scatter_dimension=1, tiled=True)  9.73 us
    all_to_all x1, starting transfers between devices, body(): lax.all_to_all(halves[None], 'freq', split_axis=1, concat_axis=0, tiled=T...  5.76 us
    gather x1, local copies, waits for them, and re-layouts, body(): own_rows = jnp.take(own_rows, pair_order, axis=1)  5.21 us
  transfers between devices with their start and end apart: 4, of which 4 were waited for; matrix products, arithmetic and copies ran while one was open for 1% of the time, Pallas kernels for 0%

commit v1 on v0

--- a/solution.py
+++ b/solution.py
@@ -6,7 +6,26 @@
 
 def body(screened, densities, pair_order, quad_index, quad_table):
     screen = screened[0]
-    own_rows = lax.all_gather(densities, "freq", axis=1, tiled=True)
+    devices, index, extent = (lax.axis_size("freq"), lax.axis_index("freq"), densities.shape[1])
+    right = [(i, (i + 1) % devices) for i in range(devices)]
+    left = [(i, (i - 1) % devices) for i in range(devices)]
+    whole = jnp.zeros(
+        (*densities.shape[:1], devices * extent, *densities.shape[1 + 1 :]), densities.dtype
+    )
+    whole = lax.dynamic_update_slice_in_dim(whole, densities, index * extent, axis=1)
+    from_left = from_right = densities
+    halfway = devices // 2
+    for step in range(1, halfway + 1):
+        from_left = lax.ppermute(from_left, "freq", right)
+        whole = lax.dynamic_update_slice_in_dim(
+            whole, from_left, (index - step) % devices * extent, axis=1
+        )
+        if step < devices - halfway:
+            from_right = lax.ppermute(from_right, "freq", left)
+            whole = lax.dynamic_update_slice_in_dim(
+                whole, from_right, (index + step) % devices * extent, axis=1
+            )
+    own_rows = whole
     own_rows = jnp.take(own_rows, pair_order, axis=1)
     product = jnp.dot(
         screen,

time: 126 us -> 116 us (0.921)
  waiting for transfers between devices: 83.6 us -> 57.1 us
  starting transfers between devices: 5.84 us -> 25.4 us
  local copies, waits for them, and re-layouts: 8.37 us -> 5.57 us
    all_gather x1 -> x0, waiting for transfers between devices: 47.8 us -> none  [body(): own_rows = lax.all_gather(densities, 'freq', axis=1, tiled=True)]
    ppermute x0 -> x7, waiting for transfers between devices: none -> 21.6 us  [the longest x4 21.6 us: body(): from_left = lax.ppermute(from_left, 'freq', right)]
    ppermute x0 -> x7, starting transfers between devices: none -> 19.6 us  [the longest x3 10.5 us: body(): from_right = lax.ppermute(from_right, 'freq', left)]
    gather x1, local copies, waits for them, and re-layouts: 5.21 us -> 2.14 us  [body(): own_rows = jnp.take(own_rows, pair_order, axis=1)]
  transfers between devices with their start and end apart: 4 -> 10, of which waited for: 4 -> 7; matrix products, arithmetic and copies ran while one was open for 1% -> 1% of each run, Pallas kernels for 0% -> 0%
where the time goes in v1:
time: 116 us
  waiting for transfers between devices  57.1 us (49%)
  starting transfers between devices  25.4 us (22%)
  between operations  13.6 us (12%)
  matrix products  12.3 us (11%)
  local copies, waits for them, and re-layouts  5.57 us (5%)
  other arithmetic  2.23 us (2%)
    ppermute x4, waiting for transfers between devices, body(): from_left = lax.ppermute(from_left, 'freq', right)  21.6 us
    all_to_all x1, waiting for transfers between devices, body(): lax.all_to_all(halves[None], 'freq', split_axis=1, concat_axis=0, tiled=T...  14.8 us
    dot_general x1, matrix products, body(): lax.dot_general(own_rows, product, (((0,), (0,)), ((), ())), preferred_el...  11.5 us
    all_gather x1, waiting for transfers between devices, body(): lax.all_gather(own_rows, 'gvec', axis=0, tiled=True)  10.9 us
    ppermute x3, starting transfers between devices, body(): from_right = lax.ppermute(from_right, 'freq', left)  10.5 us
    reduce_scatter x1, waiting for transfers between devices, body(): halves = lax.psum_scatter(kernel, 'gvec', scatter_dimension=1, tiled=True)  9.7 us
    ppermute x4, starting transfers between devices, body(): from_left = lax.ppermute(from_left, 'freq', right)  9.03 us
    all_to_all x1, starting transfers between devices, body(): lax.all_to_all(halves[None], 'freq', split_axis=1, concat_axis=0, tiled=T...  5.78 us
  transfers between devices with their start and end apart: 10, of which 7 were waited for; matrix products, arithmetic and copies ran while one was open for 1% of the time, Pallas kernels for 0%

profile of v1, /device:TPU:0, one launch (start us, length us, event | category | flops | bytes accessed | tf_op | source)
XLA Modules:
  0.0 116.1 jit_solution(4316216843737223518)
XLA Ops:
  6.5 3.0 %collective-permute-start = (bf16[1536,64]{0,1:T(8,128)(2,1)}, bf16[1536,64]{0,1:T(8,128)(2,1)S(1)}, u32[]{:S(2)}, u32[]{:S(2)}) collective-permute-start(bf16[1536,64]{0,1:T(8,128)(2,1)} %param.6), channel_id=1, source_target_pairs={{0,2},{2,4},{4,6},{6,8},{8,10},{10,12},{12,14},{14,0},{1,3},{3,5},... | collective-permute-start | bytes 589832 | tf_op jit(solution)/shard_map/ppermute | solution.py:19
  9.5 3.1 %collective-permute-start.1 = (bf16[1536,64]{0,1:T(8,128)(2,1)}, bf16[1536,64]{0,1:T(8,128)(2,1)S(1)}, u32[]{:S(2)}, u32[]{:S(2)}) collective-permute-start(bf16[1536,64]{0,1:T(8,128)(2,1)} %param.6), channel_id=1, source_target_pairs={{0,14},{2,0},{4,2},{6,4},{8,6},{10,8},{12,10},{14,12},{1,15},{3,1}... | collective-permute-start | bytes 589832 | tf_op jit(solution)/shard_map/ppermute | solution.py:24
  12.6 0.7 compare_select_fusion
  13.3 0.1 broadcast_in_dim.22
  13.4 0.0 copy-done
  13.5 4.7 %collective-permute-done = bf16[1536,64]{0,1:T(8,128)(2,1)S(1)} collective-permute-done((bf16[1536,64]{0,1:T(8,128)(2,1)}, bf16[1536,64]{0,1:T(8,128)(2,1)S(1)}, u32[]{:S(2)}, u32[]{:S(2)}) %collective-permute-start) | collective-permute-done | bytes 196640 | tf_op jit(solution)/shard_map/ppermute | solution.py:19
  18.2 2.4 %collective-permute-start.2 = (bf16[1536,64]{0,1:T(8,128)(2,1)S(1)}, bf16[1536,64]{0,1:T(8,128)(2,1)S(1)}, u32[]{:S(2)}, u32[]{:S(2)}) collective-permute-start(bf16[1536,64]{0,1:T(8,128)(2,1)S(1)} %collective-permute-done), channel_id=1, source_target_pairs={{0,2},{2,4},{4,6},{6,8},{8,10},{10,12},{12,14},{14,0},{1,3},{3,5},... | collective-permute-start | bytes 589832 | tf_op jit(solution)/shard_map/ppermute | solution.py:19
  20.6 0.0 collective-permute-done.1
  20.6 3.0 %collective-permute-start.3 = (bf16[1536,64]{0,1:T(8,128)(2,1)S(1)}, bf16[1536,64]{0,1:T(8,128)(2,1)S(1)}, u32[]{:S(2)}, u32[]{:S(2)}) collective-permute-start(bf16[1536,64]{0,1:T(8,128)(2,1)S(1)} %collective-permute-done.1), channel_id=1, source_target_pairs={{0,14},{2,0},{4,2},{6,4},{8,6},{10,8},{12,10},{14,12},{1,15},{3,1}... | collective-permute-start | bytes 589832 | tf_op jit(solution)/shard_map/ppermute | solution.py:24
  23.7 4.4 %collective-permute-done.2 = bf16[1536,64]{0,1:T(8,128)(2,1)S(1)} collective-permute-done((bf16[1536,64]{0,1:T(8,128)(2,1)S(1)}, bf16[1536,64]{0,1:T(8,128)(2,1)S(1)}, u32[]{:S(2)}, u32[]{:S(2)}) %collective-permute-start.2) | collective-permute-done | bytes 196640 | tf_op jit(solution)/shard_map/ppermute | solution.py:19
  28.1 2.5 %collective-permute-start.4 = (bf16[1536,64]{0,1:T(8,128)(2,1)S(1)}, bf16[1536,64]{0,1:T(8,128)(2,1)S(1)}, u32[]{:S(2)}, u32[]{:S(2)}) collective-permute-start(bf16[1536,64]{0,1:T(8,128)(2,1)S(1)} %collective-permute-done.2), channel_id=1, source_target_pairs={{0,2},{2,4},{4,6},{6,8},{8,10},{10,12},{12,14},{14,0},{1,3},{3,5},... | collective-permute-start | bytes 589832 | tf_op jit(solution)/shard_map/ppermute | solution.py:19
  30.6 0.0 collective-permute-done.3
  30.6 4.4 %collective-permute-start.5 = (bf16[1536,64]{0,1:T(8,128)(2,1)S(1)}, bf16[1536,64]{0,1:T(8,128)(2,1)S(1)}, u32[]{:S(2)}, u32[]{:S(2)}) collective-permute-start(bf16[1536,64]{0,1:T(8,128)(2,1)S(1)} %collective-permute-done.3), channel_id=1, source_target_pairs={{0,14},{2,0},{4,2},{6,4},{8,6},{10,8},{12,10},{14,12},{1,15},{3,1}... | collective-permute-start | bytes 589832 | tf_op jit(solution)/shard_map/ppermute | solution.py:24
  35.0 3.7 %collective-permute-done.4 = bf16[1536,64]{0,1:T(8,128)(2,1)S(1)} collective-permute-done((bf16[1536,64]{0,1:T(8,128)(2,1)S(1)}, bf16[1536,64]{0,1:T(8,128)(2,1)S(1)}, u32[]{:S(2)}, u32[]{:S(2)}) %collective-permute-start.4) | collective-permute-done | bytes 196640 | tf_op jit(solution)/shard_map/ppermute | solution.py:19
  38.7 1.2 %collective-permute-start.6 = (bf16[1536,64]{0,1:T(8,128)(2,1)S(1)}, bf16[1536,64]{0,1:T(8,128)(2,1)S(1)}, u32[]{:S(2)}, u32[]{:S(2)}) collective-permute-start(bf16[1536,64]{0,1:T(8,128)(2,1)S(1)} %collective-permute-done.4), channel_id=1, source_target_pairs={{0,2},{2,4},{4,6},{6,8},{8,10},{10,12},{12,14},{14,0},{1,3},{3,5},... | collective-permute-start | bytes 589832 | tf_op jit(solution)/shard_map/ppermute | solution.py:19
  39.9 0.0 collective-permute-done.5
  40.0 8.8 %collective-permute-done.6 = bf16[1536,64]{0,1:T(8,128)(2,1)S(1)} collective-permute-done((bf16[1536,64]{0,1:T(8,128)(2,1)S(1)}, bf16[1536,64]{0,1:T(8,128)(2,1)S(1)}, u32[]{:S(2)}, u32[]{:S(2)}) %collective-permute-start.6) | collective-permute-done | bytes 196640 | tf_op jit(solution)/shard_map/ppermute | solution.py:19
  48.8 2.1 %gather_fusion = bf16[512,1536]{1,0:T(8,128)(2,1)S(1)} fusion(bf16[1536,512]{0,1:T(8,128)(2,1)S(1)} %constant_dynamic-update-slice_fusion, s32[1024]{0:T(1024)S(1)} %pad_clamp_fusion), kind=kCustom, calls=%fused_computation | custom fusion | bytes 3147776 | tf_op jit(solution)/shard_map/jit(_take)/gather | solution.py:29
  50.9 1.4 %fusion.6 = bf16[1536,512]{0,1:T(8,128)(2,1)} fusion(bf16[512,1536]{1,0:T(8,128)(2,1)S(1)} %gather_fusion, pred[512]{0:T(512)(128)(4,1)S(1)} %compare_and_fusion), kind=kLoop, calls=%fused_computation.6 | loop fusion | flops 786432 | bytes 3146240 | tf_op jit(solution)/shard_map/jit(_take)/select_n | solution.py:29
  52.3 0.0 all-gather.2.cloned.1.call-update
  52.3 0.0 reduce-scatter.2.cloned.1.call-start
  52.4 10.9 %all-gather.2.cloned.1.call-done = bf16[3072,512]{0,1:T(8,128)(2,1)} async-done(((bf16[1536,512]{0,1:T(8,128)(2,1)}), bf16[3072,512]{0,1:T(8,128)(2,1)}) %all-gather.2.cloned.1.call-update) | async-done | bytes 3145744 | tf_op jit(solution)/shard_map/all_gather | solution.py:32
  63.3 11.5 %fusion.5 = f32[512,512]{1,0:T(8,128)} fusion(bf16[512,1536]{1,0:T(8,128)(2,1)S(1)} %gather_fusion, pred[512]{0:T(512)(128)(4,1)S(1)} %compare_and_fusion, bf16[3072,512]{0,1:T(8,128)(2,1)} %all-gather.2.cloned.1.call-done, bf16[1,1536,3072]{2,1,0:T(8,128)(2,1)} %param.5), kind=kOutput, calls=%fused_computation.5 | convolution fusion | flops 5638717440 | bytes 15204864 | tf_op jit(solution)/shard_map/dot_general | solution.py:36
  74.8 0.0 reduce-scatter.2.cloned.1.call-update
  74.9 9.7 %reduce-scatter.2.cloned.1.call-done = f32[512,256]{1,0:T(8,128)} async-done(((f32[512,512]{1,0:T(8,128)}), f32[512,256]{1,0:T(8,128)}) %reduce-scatter.2.cloned.1.call-update) | async-done | bytes 524304 | tf_op jit(solution)/shard_map/reduce_scatter | solution.py:44
  84.6 2.4 %copy.13 = f32[1,512,256]{2,0,1:T(1,128)} copy(f32[1,512,256]{2,1,0:T(8,128)} %bitcast.16) | data formatting | bytes 1048576 | tf_op jit(solution)/shard_map/broadcast_in_dim | solution.py:48
  86.9 5.8 %all-to-all-start = ((f32[1,512,256]{2,0,1:T(1,128)}), f32[1,512,256]{2,0,1:T(1,128)S(1)}, u32[]{:S(2)}, u32[]{:S(2)}) async-start(f32[1,512,256]{2,0,1:T(1,128)} %copy.13), calls=%async_computation.1 | async-start | bytes 1048576 | tf_op jit(solution)/shard_map/all_to_all | solution.py:48
  92.7 0.0 copy-done.2
  92.7 0.2 select_reduce_fusion
  92.9 14.8 %all-to-all-done = f32[1,512,256]{2,0,1:T(1,128)S(1)} async-done(((f32[1,512,256]{2,0,1:T(1,128)}), f32[1,512,256]{2,0,1:T(1,128)S(1)}, u32[]{:S(2)}, u32[]{:S(2)}) %all-to-all-start) | async-done | bytes 524320 | tf_op jit(solution)/shard_map/all_to_all | solution.py:48
  107.7 0.8 fusion.9
  108.5 0.8 copy.15
  (18 shorter events, 0.2 us)
Async XLA Ops:
  6.5 6.9 %copy-start = (bf16[1536,64]{0,1:T(8,128)(2,1)S(1)}, bf16[1536,64]{0,1:T(8,128)(2,1)}, u32[]{:S(2)}) copy-start(bf16[1536,64]{0,1:T(8,128)(2,1)} %param.6) | copy-start | bytes 589828
  6.5 7.0 %copy-start.1 = (s32[512]{0:T(512)S(1)}, s32[512]{0:T(512)}, u32[]{:S(2)}) copy-start(s32[512]{0:T(512)} %param.7) | copy-start | bytes 6148
  6.5 56.8 %all-gather.2.cloned.1.call-start = ((), (), s32[]{:S(2)}) async-start(), calls=%async_computation.2 | async-start | bytes 4718592 | tf_op jit(solution)/shard_map/all_gather | solution.py:32
  6.5 11.7 %collective-permute-start = (bf16[1536,64]{0,1:T(8,128)(2,1)}, bf16[1536,64]{0,1:T(8,128)(2,1)S(1)}, u32[]{:S(2)}, u32[]{:S(2)}) collective-permute-start(bf16[1536,64]{0,1:T(8,128)(2,1)} %param.6), channel_id=1, source_target_pairs={{0,2},{2,4},{4,6},{6,8},{8,10},{10,12},{12,14},{14,0},{1,3},{3,5},... | collective-permute-start | bytes 589832 | tf_op jit(solution)/shard_map/ppermute | solution.py:19
  9.5 11.1 %collective-permute-start.1 = (bf16[1536,64]{0,1:T(8,128)(2,1)}, bf16[1536,64]{0,1:T(8,128)(2,1)S(1)}, u32[]{:S(2)}, u32[]{:S(2)}) collective-permute-start(bf16[1536,64]{0,1:T(8,128)(2,1)} %param.6), channel_id=1, source_target_pairs={{0,14},{2,0},{4,2},{6,4},{8,6},{10,8},{12,10},{14,12},{1,15},{3,1}... | collective-permute-start | bytes 589832 | tf_op jit(solution)/shard_map/ppermute | solution.py:24
  18.2 9.9 %collective-permute-start.2 = (bf16[1536,64]{0,1:T(8,128)(2,1)S(1)}, bf16[1536,64]{0,1:T(8,128)(2,1)S(1)}, u32[]{:S(2)}, u32[]{:S(2)}) collective-permute-start(bf16[1536,64]{0,1:T(8,128)(2,1)S(1)} %collective-permute-done), channel_id=1, source_target_pairs={{0,2},{2,4},{4,6},{6,8},{8,10},{10,12},{12,14},{14,0},{1,3},{3,5},... | collective-permute-start | bytes 589832 | tf_op jit(solution)/shard_map/ppermute | solution.py:19
  20.6 10.0 %collective-permute-start.3 = (bf16[1536,64]{0,1:T(8,128)(2,1)S(1)}, bf16[1536,64]{0,1:T(8,128)(2,1)S(1)}, u32[]{:S(2)}, u32[]{:S(2)}) collective-permute-start(bf16[1536,64]{0,1:T(8,128)(2,1)S(1)} %collective-permute-done.1), channel_id=1, source_target_pairs={{0,14},{2,0},{4,2},{6,4},{8,6},{10,8},{12,10},{14,12},{1,15},{3,1}... | collective-permute-start | bytes 589832 | tf_op jit(solution)/shard_map/ppermute | solution.py:24
  28.1 10.6 %collective-permute-start.4 = (bf16[1536,64]{0,1:T(8,128)(2,1)S(1)}, bf16[1536,64]{0,1:T(8,128)(2,1)S(1)}, u32[]{:S(2)}, u32[]{:S(2)}) collective-permute-start(bf16[1536,64]{0,1:T(8,128)(2,1)S(1)} %collective-permute-done.2), channel_id=1, source_target_pairs={{0,2},{2,4},{4,6},{6,8},{8,10},{10,12},{12,14},{14,0},{1,3},{3,5},... | collective-permute-start | bytes 589832 | tf_op jit(solution)/shard_map/ppermute | solution.py:19
  30.6 9.3 %collective-permute-start.5 = (bf16[1536,64]{0,1:T(8,128)(2,1)S(1)}, bf16[1536,64]{0,1:T(8,128)(2,1)S(1)}, u32[]{:S(2)}, u32[]{:S(2)}) collective-permute-start(bf16[1536,64]{0,1:T(8,128)(2,1)S(1)} %collective-permute-done.3), channel_id=1, source_target_pairs={{0,14},{2,0},{4,2},{6,4},{8,6},{10,8},{12,10},{14,12},{1,15},{3,1}... | collective-permute-start | bytes 589832 | tf_op jit(solution)/shard_map/ppermute | solution.py:24
  38.7 10.0 %collective-permute-start.6 = (bf16[1536,64]{0,1:T(8,128)(2,1)S(1)}, bf16[1536,64]{0,1:T(8,128)(2,1)S(1)}, u32[]{:S(2)}, u32[]{:S(2)}) collective-permute-start(bf16[1536,64]{0,1:T(8,128)(2,1)S(1)} %collective-permute-done.4), channel_id=1, source_target_pairs={{0,2},{2,4},{4,6},{6,8},{8,10},{10,12},{12,14},{14,0},{1,3},{3,5},... | collective-permute-start | bytes 589832 | tf_op jit(solution)/shard_map/ppermute | solution.py:19
  52.3 32.2 %reduce-scatter.2.cloned.1.call-start = ((), (), s32[]{:S(2)}) async-start(), calls=%async_computation.3 | async-start | bytes 1572864 | tf_op jit(solution)/shard_map/reduce_scatter | solution.py:44
  74.8 17.9 %copy-start.2 = (s32[4,8]{1,0:T(4,128)S(1)}, s32[4,8]{1,0:T(4,128)}, u32[]{:S(2)}) copy-start(s32[4,8]{1,0:T(4,128)} %param.8) | copy-start | bytes 388
  74.8 17.9 %copy-start.3 = (f32[64]{0:T(128)S(1)}, f32[64]{0:T(128)}, u32[]{:S(2)}) copy-start(f32[64]{0:T(128)} %param.9) | copy-start | bytes 772
  86.9 20.8 %all-to-all-start = ((f32[1,512,256]{2,0,1:T(1,128)}), f32[1,512,256]{2,0,1:T(1,128)S(1)}, u32[]{:S(2)}, u32[]{:S(2)}) async-start(f32[1,512,256]{2,0,1:T(1,128)} %copy.13), calls=%async_computation.1 | async-start | bytes 1048576 | tf_op jit(solution)/shard_map/all_to_all | solution.py:48
Sparse Core Ops, SparseCore 0:
  52.5 10.8 all-gather.1
  75.0 9.5 reduce-scatter.1
